TPU v7x, 32 devices: a whole 2x2x4 slice. The times are simulated.
32 devices in a mesh: dp: 2 (over x), row: 4 (over z), col: 4 (over y, core).
Axes of the slice: x: 2, y: 2, z: 4, core: 2. Of those that a mesh axis runs over, the one named last changes fastest.
Arguments:
- layer_input: bfloat16 [2048, 2048], P(('dp', 'col'), 'row'), may hold values from -6 to 6
- cotangent: bfloat16 [2048, 2048], P(('dp', 'col'), 'row'), may hold values from -6 to 6
- w_query: bfloat16 [2048, 2048], P('row', 'col'), may hold values from -0.125 to 0.125
- key_matrix: bfloat16 [2048, 1024], P('row', 'col'), may hold values from -0.125 to 0.125
- value_matrix: bfloat16 [2048, 1024], P('row', 'col'), may hold values from -0.125 to 0.125
- w_output: bfloat16 [2048, 2048], P('col', 'row'), may hold values from -1 to 1
- w_gate: bfloat16 [2048, 6144], P('row', 'col'), may hold values from -0.125 to 0.125
- w_up: bfloat16 [2048, 6144], P('row', 'col'), may hold values from -0.125 to 0.125
- w_down: bfloat16 [6144, 2048], P('col', 'row'), may hold values from -0.078125 to 0.078125
- attn_gain: float32 [2048], P('row'), may hold values from 0.5 to 1.5
- mlp_gain: float32 [2048], P('row'), may hold values from 0.5 to 1.5
- query_gain: float32 [128], replicated, may hold values from 0.5 to 1.5
- key_gain: float32 [128], replicated, may hold values from 0.5 to 1.5
- segment_ids: int32 [8, 256], P(('dp', 'row')), may hold values from 0 to 3, never falling along the last dimension, each value on 1 to 128 neighbouring positions
Outputs:
- block_out: bfloat16 [2048, 2048], P(('dp', 'col'), 'row')
- input_grad: float32 [2048, 2048], P(('dp', 'col'), 'row')
- grad_query: float32 [2048, 2048], P('row', 'col')
- grad_key: float32 [2048, 1024], P('row', 'col')
- grad_value: float32 [2048, 1024], P('row', 'col')
- grad_output: float32 [2048, 2048], P('col', 'row')
- grad_gate: float32 [2048, 6144], P('row', 'col')
- grad_up: float32 [2048, 6144], P('row', 'col')
- grad_down: float32 [6144, 2048], P('col', 'row')
- gain_attn: float32 [2048], replicated
- gain_mlp: float32 [2048], replicated
- gain_query: float32 [128], replicated
- gain_key: float32 [128], replicated
All inputs are finite; a program needn't handle non-finite values.
Results may differ from a plain program's by a relative error of at most 0.015.
Values may be sent and summed in bfloat16 or wider, within the bound.
A program may use at most 128 MiB of HBM per device.

v0:
```python
import jax
import jax.numpy as jnp
from jax import lax
from jax.sharding import PartitionSpec as P

MODEL_WIDTH = 2048
HEAD_SIZE = 128
EPSILON = 1e-06
THETA = 1000000.0


def positions_of(segment):
    length = segment.shape[0]
    index = jnp.arange(length, dtype=jnp.int32)
    change = jnp.concatenate(
        [jnp.ones((1,), jnp.int32), (segment[1:] != segment[:-1]).astype(jnp.int32)]
    )
    starts = lax.cummax(jnp.where(change > 0, index, jnp.zeros_like(index)), axis=0)
    return index - starts


def rope_tables(segment, width):
    half = width // 2
    inverse = jnp.power(THETA, -(jnp.arange(half, dtype=jnp.float32) * (2.0 / width)))
    angle = positions_of(segment).astype(jnp.float32)[:, None] * inverse[None, :]
    return (jnp.cos(angle), jnp.sin(angle))


def rotate(field, cosine, sine):
    half = field.shape[-1] // 2
    first = field[..., :half]
    second = field[..., half:]
    cos_b = cosine[:, None, :]
    sin_b = sine[:, None, :]
    return jnp.concatenate(
        [first * cos_b - second * sin_b, second * cos_b + first * sin_b], axis=-1
    )


def unrotate(grad, cosine, sine):
    half = grad.shape[-1] // 2
    first = grad[..., :half]
    second = grad[..., half:]
    cos_b = cosine[:, None, :]
    sin_b = sine[:, None, :]
    return jnp.concatenate(
        [first * cos_b + second * sin_b, second * cos_b - first * sin_b], axis=-1
    )


def head_norm(field, gain):
    scale = lax.rsqrt(jnp.mean(field * field, axis=-1, keepdims=True) + EPSILON)
    unit = field * scale
    return (unit * gain, unit, scale)


def head_norm_back(grad, unit, scale, gain):
    inner = grad * gain
    back = scale * (inner - unit * jnp.mean(inner * unit, axis=-1, keepdims=True))
    return (back, jnp.sum(grad * unit, axis=(0, 1)))


def mix(form, left, right):
    return jnp.einsum(form, left, right, preferred_element_type=jnp.float32)


def score_mask(segment, start, block):
    length = segment.shape[0]
    query_index = start + jnp.arange(block, dtype=jnp.int32)
    key_index = jnp.arange(length, dtype=jnp.int32)
    return (segment[:, None] == segment[None, :]) & (key_index[None, :] <= query_index[:, None])


def attend(query, key_rows, value_rows, segment):
    length, heads, width = query.shape
    groups = key_rows.shape[1]
    group_factor = heads // groups
    block = min(512, length)
    blocks = length // block
    scale = width ** (-0.5)
    grouped = query.reshape(blocks, block, groups, group_factor, width)
    starts = jnp.arange(blocks, dtype=jnp.int32) * block

    def one_block(item):
        query_block, start = item
        scores = mix("qgrd,kgd->grqk", query_block, key_rows) * scale
        allowed = score_mask(segment, start, block)
        scores = jnp.where(allowed[None, None], scores, -1e30)
        top = jnp.max(scores, axis=-1, keepdims=True)
        weights = jnp.exp(scores - top)
        total = jnp.sum(weights, axis=-1, keepdims=True)
        probs = (weights / total).astype(jnp.bfloat16)
        result = mix("grqk,kgd->qgrd", probs, value_rows)
        return (result.astype(jnp.bfloat16), (top + jnp.log(total))[..., 0])

    results, log_total = lax.map(one_block, (grouped, starts))
    return (results.reshape(length, heads * width), log_total)


def attend_back(query, key_rows, value_rows, segment, mixed, grad_mixed, log_total):
    length, heads, width = query.shape
    groups = key_rows.shape[1]
    group_factor = heads // groups
    block = min(512, length)
    blocks = length // block
    scale = width ** (-0.5)
    delta = jnp.sum(
        grad_mixed.astype(jnp.float32).reshape(length, heads, width)
        * mixed.astype(jnp.float32).reshape(length, heads, width),
        axis=-1,
    )
    delta = jnp.transpose(delta.reshape(blocks, block, groups, group_factor), (0, 2, 3, 1))
    grouped = query.reshape(blocks, block, groups, group_factor, width)
    grouped_grad = grad_mixed.reshape(blocks, block, groups, group_factor, width)
    starts = jnp.arange(blocks, dtype=jnp.int32) * block

    def one_block(carry, item):
        grad_keys, value_gradients = carry
        query_block, grad_block, total_block, delta_block, start = item
        scores = mix("qgrd,kgd->grqk", query_block, key_rows) * scale
        allowed = score_mask(segment, start, block)
        scores = jnp.where(allowed[None, None], scores, -1e30)
        probs = jnp.exp(scores - total_block[..., None])
        value_gradients = value_gradients + mix(
            "grqk,qgrd->kgd", probs.astype(jnp.bfloat16), grad_block
        )
        grad_probs = mix("qgrd,kgd->grqk", grad_block, value_rows)
        grad_scores = (probs * (grad_probs - delta_block[..., None])).astype(jnp.bfloat16)
        grad_query = mix("grqk,kgd->qgrd", grad_scores, key_rows) * scale
        grad_keys = grad_keys + mix("grqk,qgrd->kgd", grad_scores, query_block) * scale
        return ((grad_keys, value_gradients), grad_query)

    empty = jnp.zeros((length, groups, width), jnp.float32)
    (grad_keys, value_gradients), grad_query = lax.scan(
        one_block, (empty, empty), (grouped, grouped_grad, log_total, delta, starts)
    )
    return (grad_query.reshape(length, heads, width), grad_keys, value_gradients)


def silu_parts(gate):
    sigma = jax.nn.sigmoid(gate)
    return (gate * sigma, sigma * (1.0 + gate * (1.0 - sigma)))


def matrix_result(left, right, flipped):
    if flipped:
        return lax.dot_general(
            left, right, (((1,), (1,)), ((), ())), preferred_element_type=jnp.float32
        )
    return jnp.dot(left, right, preferred_element_type=jnp.float32)


def weight_term(left, right):
    return lax.dot_general(
        left, right, (((0,), (0,)), ((), ())), preferred_element_type=jnp.float32
    )


def row_stats(partial_value):
    return lax.psum(partial_value, "row")


def gather_cols(piece):
    return lax.all_gather(piece, "col", axis=0, tiled=True)


def gather_rows(piece):
    return lax.all_gather(piece, "row", axis=0, tiled=True)


def row_product(gathered, weight, flipped):
    return lax.psum_scatter(
        matrix_result(gathered, weight, flipped), "row", scatter_dimension=0, tiled=True
    )


def col_sum(gathered, weight, flipped):
    return lax.psum_scatter(
        matrix_result(gathered, weight, flipped), "col", scatter_dimension=0, tiled=True
    )


def per_device(
    layer_input,
    cotangent,
    w_query,
    key_matrix,
    value_matrix,
    w_output,
    w_gate,
    w_up,
    w_down,
    attn_gain,
    mlp_gain,
    query_gain,
    key_gain,
    segment_ids,
):
    segment = segment_ids[0]
    length = segment.shape[0]
    feat_rows = layer_input.shape[1]
    query_width = w_query.shape[1]
    key_width = key_matrix.shape[1]
    ff_local = w_gate.shape[1]
    cosine, sine = rope_tables(segment, HEAD_SIZE)
    w_joint = jnp.concatenate([w_query, key_matrix, value_matrix], axis=1)
    w_pair = jnp.concatenate([w_gate, w_up], axis=1)
    inputs = layer_input.astype(jnp.float32)
    scale_in = lax.rsqrt(row_stats(jnp.sum(inputs * inputs, axis=-1)) / MODEL_WIDTH + EPSILON)[
        :, None
    ]
    unit_in = inputs * scale_in
    normalized_input = (unit_in * attn_gain).astype(jnp.bfloat16)
    gathered_in = gather_cols(normalized_input)
    projected = row_product(gathered_in, w_joint, False)
    query = projected[:, :query_width].reshape(length, query_width // HEAD_SIZE, HEAD_SIZE)
    key_rows = projected[:, query_width : query_width + key_width].reshape(
        length, key_width // HEAD_SIZE, HEAD_SIZE
    )
    value_rows = (
        projected[:, query_width + key_width :]
        .astype(jnp.bfloat16)
        .reshape(length, key_width // HEAD_SIZE, HEAD_SIZE)
    )
    query_norm, query_unit, query_scale = head_norm(query, query_gain)
    key_norm, key_unit, key_scale = head_norm(key_rows, key_gain)
    query_rot = rotate(query_norm, cosine, sine).astype(jnp.bfloat16)
    key_rot = rotate(key_norm, cosine, sine).astype(jnp.bfloat16)
    mixed, log_total = attend(query_rot, key_rot, value_rows, segment)
    gathered_mix = gather_rows(mixed)
    hidden = inputs + col_sum(gathered_mix, w_output, False)
    scale_mid = lax.rsqrt(row_stats(jnp.sum(hidden * hidden, axis=-1)) / MODEL_WIDTH + EPSILON)[
        :, None
    ]
    unit_mid = hidden * scale_mid
    normed_mid = (unit_mid * mlp_gain).astype(jnp.bfloat16)
    gathered_mid = gather_cols(normed_mid)
    joined = row_product(gathered_mid, w_pair, False)
    gate = joined[:, :ff_local]
    upward = joined[:, ff_local:]
    silu, slope = silu_parts(gate)
    active = (silu * upward).astype(jnp.bfloat16)
    gathered_act = gather_rows(active)
    block_out = (hidden + col_sum(gathered_act, w_down, False)).astype(jnp.bfloat16)
    gathered_cot = gather_cols(cotangent)
    grad_active = row_product(gathered_cot, w_down, True)
    grad_down = weight_term(gathered_act, gathered_cot)
    grad_pair_in = jnp.concatenate(
        [
            (grad_active * upward * slope).astype(jnp.bfloat16),
            (grad_active * silu).astype(jnp.bfloat16),
        ],
        axis=1,
    )
    gathered_pair = gather_rows(grad_pair_in)
    grad_mid = col_sum(gathered_pair, w_pair, True)
    grad_pair = weight_term(gathered_mid, gathered_pair)
    inner_mid = grad_mid * mlp_gain
    gain_mid = jnp.sum(grad_mid * unit_mid, axis=0)
    mean_mid = row_stats(jnp.sum(inner_mid * unit_mid, axis=-1))[:, None] / MODEL_WIDTH
    grad_hidden = cotangent.astype(jnp.float32) + scale_mid * (inner_mid - unit_mid * mean_mid)
    grad_attn = grad_hidden.astype(jnp.bfloat16)
    gathered_attn = gather_cols(grad_attn)
    grad_mixed = row_product(gathered_attn, w_output, True).astype(jnp.bfloat16)
    grad_output = weight_term(gathered_mix, gathered_attn)
    grad_query_rot, grad_key_rot, value_gradients = attend_back(
        query_rot, key_rot, value_rows, segment, mixed, grad_mixed, log_total
    )
    grad_query_raw, gain_query = head_norm_back(
        unrotate(grad_query_rot, cosine, sine), query_unit, query_scale, query_gain
    )
    unrotated_key_gradient, gain_key = head_norm_back(
        unrotate(grad_key_rot, cosine, sine), key_unit, key_scale, key_gain
    )
    grad_joint_in = jnp.concatenate(
        [
            grad_query_raw.reshape(length, query_width).astype(jnp.bfloat16),
            unrotated_key_gradient.reshape(length, key_width).astype(jnp.bfloat16),
            value_gradients.reshape(length, key_width).astype(jnp.bfloat16),
        ],
        axis=1,
    )
    gathered_joint = gather_rows(grad_joint_in)
    grad_in_norm = col_sum(gathered_joint, w_joint, True)
    grad_joint = weight_term(gathered_in, gathered_joint)
    grad_joint, grad_output, grad_pair, grad_down = (
        lax.psum(grad_joint.astype(jnp.bfloat16), "dp").astype(jnp.float32),
        lax.psum(grad_output.astype(jnp.bfloat16), "dp").astype(jnp.float32),
        lax.psum(grad_pair.astype(jnp.bfloat16), "dp").astype(jnp.float32),
        lax.psum(grad_down.astype(jnp.bfloat16), "dp").astype(jnp.float32),
    )
    inner_in = grad_in_norm * attn_gain
    gain_in = jnp.sum(grad_in_norm * unit_in, axis=0)
    mean_in = row_stats(jnp.sum(inner_in * unit_in, axis=-1))[:, None] / MODEL_WIDTH
    input_grad = grad_hidden + scale_in * (inner_in - unit_in * mean_in)
    offset = lax.axis_index("row") * feat_rows
    gain_in_full = lax.dynamic_update_slice(
        jnp.zeros((MODEL_WIDTH,), jnp.float32), gain_in, (offset,)
    )
    gain_mid_full = lax.dynamic_update_slice(
        jnp.zeros((MODEL_WIDTH,), jnp.float32), gain_mid, (offset,)
    )
    gain_attn, gain_mlp, gain_q, gain_k = lax.psum(
        (gain_in_full, gain_mid_full, gain_query, gain_key), ("dp", "row", "col")
    )
    return (
        block_out,
        input_grad,
        grad_joint[:, :query_width],
        grad_joint[:, query_width : query_width + key_width],
        grad_joint[:, query_width + key_width :],
        grad_output,
        grad_pair[:, :ff_local],
        grad_pair[:, ff_local:],
        grad_down,
        gain_attn,
        gain_mlp,
        gain_q,
        gain_k,
    )


def solution(mesh):
    return jax.shard_map(
        per_device,
        mesh=mesh,
        in_specs=(
            P(("dp", "col"), "row"),
            P(("dp", "col"), "row"),
            P("row", "col"),
            P("row", "col"),
            P("row", "col"),
            P("col", "row"),
            P("row", "col"),
            P("row", "col"),
            P("col", "row"),
            P("row"),
            P("row"),
            P(),
            P(),
            P(("dp", "row"), None),
        ),
        out_specs=(
            P(("dp", "col"), "row"),
            P(("dp", "col"), "row"),
            P("row", "col"),
            P("row", "col"),
            P("row", "col"),
            P("col", "row"),
            P("row", "col"),
            P("row", "col"),
            P("col", "row"),
            P(),
            P(),
            P(),
            P(),
        ),
        check_vma=False,
    )
```

profile of v0, /device:TPU:0, one launch (start us, length us, event | category | flops | bytes accessed | tf_op | source)
XLA Modules:
  0.0 1177.3 jit_solution(7358234763588839211)
XLA Ops:
  8.5 13.5 %psum.84 = f32[256]{0:T(256)S(1)} all-reduce(f32[256]{0:T(256)S(1)} %fusion.21), channel_id=1, replica_groups=mesh['dp'=2,'row'=4,'col'=4] {'row'}, use_global_device_ids=true, to_apply=%region_1.2 | all-reduce | flops 256 | bytes 2048 | tf_op jit(solution)/shard_map/psum | solution.py:160
  25.0 13.8 %all-gather.9.cloned.1.call-done = bf16[1024,512]{1,0:T(8,128)(2,1)} async-done(((bf16[256,512]{1,0:T(8,128)(2,1)}), bf16[1024,512]{1,0:T(8,128)(2,1)}) %all-gather.9.cloned.1.call-update) | async-done | bytes 1048592 | tf_op jit(solution)/shard_map/all_gather | solution.py:164
  46.0 74.3 %reduce-scatter.9.cloned.1.call-done = f32[256,1024]{1,0:T(8,128)} async-done(((f32[1024,1024]{1,0:T(8,128)}), f32[256,1024]{1,0:T(8,128)}) %reduce-scatter.9.cloned.1.call-update) | async-done | bytes 1048592 | tf_op jit(solution)/shard_map/reduce_scatter | solution.py:172
  130.9 30.6 %all-gather.11.cloned.1.call-done = bf16[1024,512]{0,1:T(8,128)(2,1)} async-done(((bf16[256,512]{0,1:T(8,128)(2,1)}), bf16[1024,512]{0,1:T(8,128)(2,1)}) %all-gather.11.cloned.1.call-update) | async-done | bytes 1048592 | tf_op jit(solution)/shard_map/all_gather | solution.py:168
  165.4 29.0 %reduce-scatter.11.cloned.1.call-done = f32[256,512]{1,0:T(8,128)} async-done(((f32[1024,512]{1,0:T(8,128)}), f32[256,512]{1,0:T(8,128)}) %reduce-scatter.11.cloned.1.call-update) | async-done | bytes 524304 | tf_op jit(solution)/shard_map/reduce_scatter | solution.py:178
  195.6 12.2 %psum.85 = f32[256]{0:T(256)} all-reduce(f32[256]{0:T(256)S(1)} %get-tuple-element.81), channel_id=1, replica_groups=mesh['dp'=2,'row'=4,'col'=4] {'row'}, use_global_device_ids=true, to_apply=%region_11.12 | all-reduce | flops 256 | bytes 2048 | tf_op jit(solution)/shard_map/psum | solution.py:160
  212.5 5.6 fusion.52
  222.3 9.0 all-gather.13.cloned.1.call-done
  231.3 11.0 fusion.50
  242.5 101.9 %reduce-scatter.17.cloned.1.call-done = f32[256,1536]{1,0:T(8,128)} async-done(((f32[1024,1536]{1,0:T(8,128)}), f32[256,1536]{1,0:T(8,128)}) %reduce-scatter.17.cloned.1.call-update) | async-done | bytes 1572880 | tf_op jit(solution)/shard_map/reduce_scatter | solution.py:172
  344.4 214.8 %reduce-scatter.13.cloned.1.call-done = f32[256,3072]{1,0:T(8,128)} async-done(((f32[1024,3072]{1,0:T(8,128)}), f32[256,3072]{1,0:T(8,128)}) %reduce-scatter.13.cloned.1.call-update) | async-done | bytes 3145744 | tf_op jit(solution)/shard_map/reduce_scatter | solution.py:172
  564.8 116.5 %all-gather.19.cloned.1.call-done = bf16[1024,3072]{1,0:T(8,128)(2,1)} async-done(((bf16[256,3072]{1,0:T(8,128)(2,1)}), bf16[1024,3072]{1,0:T(8,128)(2,1)}) %all-gather.19.cloned.1.call-update) | async-done | bytes 6291472 | tf_op jit(solution)/shard_map/all_gather | solution.py:168
  681.3 8.5 fusion.53
  689.8 29.5 %reduce-scatter.19.cloned.1.call-done = f32[256,512]{1,0:T(8,128)} async-done(((f32[1024,512]{1,0:T(8,128)}), f32[256,512]{1,0:T(8,128)}) %reduce-scatter.19.cloned.1.call-update) | async-done | bytes 524304 | tf_op jit(solution)/shard_map/reduce_scatter | solution.py:178
  721.2 12.3 %psum.86 = f32[256]{0:T(256)} all-reduce(f32[256]{0:T(256)} %get-tuple-element.57), channel_id=1, replica_groups=mesh['dp'=2,'row'=4,'col'=4] {'row'}, use_global_device_ids=true, to_apply=%region_17.18 | all-reduce | flops 256 | bytes 2048 | tf_op jit(solution)/shard_map/psum | solution.py:160
  736.8 14.0 %all-gather.21.cloned.1.call-done = bf16[1024,512]{1,0:T(8,128)(2,1)} async-done(((bf16[256,512]{1,0:T(8,128)(2,1)}), bf16[1024,512]{1,0:T(8,128)(2,1)}) %all-gather.21.cloned.1.call-update) | async-done | bytes 1048592 | tf_op jit(solution)/shard_map/all_gather | solution.py:164
  757.7 40.4 %reduce-scatter.21.cloned.1.call-done = f32[256,512]{1,0:T(8,128)} async-done(((f32[1024,512]{1,0:T(8,128)}), f32[256,512]{1,0:T(8,128)}) %reduce-scatter.21.cloned.1.call-update) | async-done | bytes 524304 | tf_op jit(solution)/shard_map/reduce_scatter | solution.py:172
  827.4 44.4 %all-gather.23.cloned.1.call-done = bf16[1024,1024]{1,0:T(8,128)(2,1)} async-done(((bf16[256,1024]{1,0:T(8,128)(2,1)}), bf16[1024,1024]{1,0:T(8,128)(2,1)}) %all-gather.23.cloned.1.call-update) | async-done | bytes 2097168 | tf_op jit(solution)/shard_map/all_gather | solution.py:168
  876.5 59.5 %all-gather.15.cloned.1.call-done = bf16[1024,1536]{1,0:T(8,128)(2,1)} async-done(((bf16[256,1536]{1,0:T(8,128)(2,1)}), bf16[1024,1536]{1,0:T(8,128)(2,1)}) %all-gather.15.cloned.1.call-update) | async-done | bytes 3145744 | tf_op jit(solution)/shard_map/all_gather | solution.py:168
  947.5 7.8 convolution_convert_fusion
  960.5 8.4 reduce-scatter.23.cloned.1.call-done
  970.4 11.6 psum.87
  982.1 37.7 %all-reduce = (f32[2048]{0:T(1024)}, f32[2048]{0:T(1024)}, f32[128]{0:T(128)}, f32[128]{0:T(128)}) all-reduce(f32[2048]{0:T(1024)S(1)} %dynamic_update_slice.15, f32[2048]{0:T(1024)S(1)} %dynamic_update_slice.16, f32[128]{0:T(128)S(1)} %bitcast_reduce_fusion, ...), channel_id=1, replica_groups=mesh['dp'=2,'row'=4,'col'=4] {'dp','row','col'}, use_global_device_ids=true, to_apply=%region_30.31 | all-reduce | flops 4352 | bytes 34816 | tf_op jit(solution)/shard_map/psum | solution.py:303
  1022.1 138.5 %all-reduce.4.cloned.1.call-done = (bf16[512,1024]{1,0:T(8,128)(2,1)}, bf16[512,512]{1,0:T(8,128)(2,1)}, bf16[512,3072]{1,0:T(8,128)(2,1)}, bf16[1536,512]{1,0:T(8,128)(2,1)}) async-done(((bf16[512,1024]{1,0:T(8,128)(2,1)}, bf16[512,512]{1,0:T(8,128)(2,1)}, bf16[512,3072]{1,0:T(8,128)(2,1)}, bf16[1536,512]{1,0:T(8,128)(2,1)}), (bf16[512,1024]{1,0:T(8,128)(2,1)}, bf16[512,512]{1,0:T(8,128)(2,1)}, ...) | async-done | bytes 6291472 | tf_op jit(solution)/shard_map/psum | solution.py:287
  (247 shorter events, 118.0 us)
Async XLA Ops:
  7.2 205.4 %copy-start = (bf16[1536,512]{1,0:T(8,128)(2,1)S(1)}, bf16[1536,512]{1,0:T(8,128)(2,1)}, u32[]{:S(2)}) copy-start(bf16[1536,512]{1,0:T(8,128)(2,1)} %param.22) | copy-start | bytes 4718596
  7.2 31.6 %all-gather.9.cloned.1.call-start = ((), (), s32[]{:S(2)}) async-start(), calls=%async_computation.8 | async-start | bytes 1310720 | tf_op jit(solution)/shard_map/all_gather | solution.py:164
  23.8 96.5 %reduce-scatter.9.cloned.1.call-start = ((), (), s32[]{:S(2)}) async-start(), calls=%async_computation.9 | async-start | bytes 5242880 | tf_op jit(solution)/shard_map/reduce_scatter | solution.py:172
  43.3 78.7 %copy-start.48 = (f32[128]{0:T(128)S(1)}, f32[128]{0:T(128)}, u32[]{:S(2)}) copy-start(f32[128]{0:T(128)} %param.25) | copy-start | bytes 1540
  43.3 118.1 %all-gather.11.cloned.1.call-start = ((), (), s32[]{:S(2)}) async-start(), calls=%async_computation.10 | async-start | bytes 1310720 | tf_op jit(solution)/shard_map/all_gather | solution.py:168
  46.0 80.1 %copy-start.7 = (f32[256,64]{1,0:T(8,128)}, f32[256,64]{1,0:T(8,128)S(1)}, u32[]{:S(2)}) copy-start(f32[256,64]{1,0:T(8,128)S(1)} %get-tuple-element.111) | copy-start | bytes 196612
  130.8 63.6 %reduce-scatter.11.cloned.1.call-start = ((), (), s32[]{:S(2)}) async-start(), calls=%async_computation.11 | async-start | bytes 2621440 | tf_op jit(solution)/shard_map/reduce_scatter | solution.py:178
  164.8 47.8 %all-gather.17.cloned.1.call-start = ((), (), s32[]{:S(2)}) async-start(), calls=%async_computation.16 | async-start | bytes 1310720 | tf_op jit(solution)/shard_map/all_gather | solution.py:164
  165.3 65.9 %all-gather.13.cloned.1.call-start = ((), (), s32[]{:S(2)}) async-start(), calls=%async_computation.12 | async-start | bytes 1310720 | tf_op jit(solution)/shard_map/all_gather | solution.py:164
  208.5 525.7 %copy-start.37 = (f32[256]{0:T(256)}, f32[256]{0:T(256)S(1)}, u32[]{:S(2)}) copy-start(f32[256]{0:T(256)S(1)} %add_rsqrt_fusion.2) | copy-start | bytes 3076
  209.4 135.0 %reduce-scatter.17.cloned.1.call-start = ((), (), s32[]{:S(2)}) async-start(), calls=%async_computation.17 | async-start | bytes 7864320 | tf_op jit(solution)/shard_map/reduce_scatter | solution.py:172
  218.2 341.0 %reduce-scatter.13.cloned.1.call-start = ((), (), s32[]{:S(2)}) async-start(), calls=%async_computation.13 | async-start | bytes 15728640 | tf_op jit(solution)/shard_map/reduce_scatter | solution.py:172
  242.3 439.0 %all-gather.19.cloned.1.call-start = ((), (), s32[]{:S(2)}) async-start(), calls=%async_computation.18 | async-start | bytes 7864320 | tf_op jit(solution)/shard_map/all_gather | solution.py:168
  564.8 154.5 %reduce-scatter.19.cloned.1.call-start = ((), (), s32[]{:S(2)}) async-start(), calls=%async_computation.19 | async-start | bytes 2621440 | tf_op jit(solution)/shard_map/reduce_scatter | solution.py:178
  689.8 61.1 %all-gather.21.cloned.1.call-start = ((), (), s32[]{:S(2)}) async-start(), calls=%async_computation.20 | async-start | bytes 1310720 | tf_op jit(solution)/shard_map/all_gather | solution.py:164
  736.8 61.3 %reduce-scatter.21.cloned.1.call-start = ((), (), s32[]{:S(2)}) async-start(), calls=%async_computation.21 | async-start | bytes 2621440 | tf_op jit(solution)/shard_map/reduce_scatter | solution.py:172
  754.3 117.5 %all-gather.23.cloned.1.call-start = ((), (), s32[]{:S(2)}) async-start(), calls=%async_computation.22 | async-start | bytes 2621440 | tf_op jit(solution)/shard_map/all_gather | solution.py:168
  826.7 109.3 %all-gather.15.cloned.1.call-start = ((), (), s32[]{:S(2)}) async-start(), calls=%async_computation.14 | async-start | bytes 3932160 | tf_op jit(solution)/shard_map/all_gather | solution.py:168
  827.3 141.5 %reduce-scatter.23.cloned.1.call-start = ((), (), s32[]{:S(2)}) async-start(), calls=%async_computation.23 | async-start | bytes 2621440 | tf_op jit(solution)/shard_map/reduce_scatter | solution.py:178
  876.2 143.5 %reduce-scatter.15.cloned.1.call-start = ((), (), s32[]{:S(2)}) async-start(), calls=%async_computation.15 | async-start | bytes 2621440 | tf_op jit(solution)/shard_map/reduce_scatter | solution.py:178
  941.1 219.5 %all-reduce.4.cloned.1.call-start = ((), (), s32[]{:S(2)}) async-start(), calls=%async_computation.24 | async-start | bytes 12582912 | tf_op jit(solution)/shard_map/psum | solution.py:287
  959.6 60.2 %copy-start.5 = (f32[256,512]{1,0:T(8,128)S(1)}, f32[256,512]{1,0:T(8,128)}, u32[]{:S(2)}) copy-start(f32[256,512]{1,0:T(8,128)} %reduce-scatter.19.cloned.1.call-done) | copy-start | bytes 1572868
  959.6 60.2 %copy-start.16 = (bf16[256,512]{1,0:T(8,128)(2,1)S(1)}, bf16[256,512]{1,0:T(8,128)(2,1)}, u32[]{:S(2)}) copy-start(bf16[256,512]{1,0:T(8,128)(2,1)} %param.15) | copy-start | bytes 786436
  959.6 60.2 %copy-start.38 = (f32[256]{0:T(256)S(1)}, f32[256]{0:T(256)}, u32[]{:S(2)}) copy-start(f32[256]{0:T(256)} %copy-done.37) | copy-start | bytes 3076
  (49 other events, 407.0 us)
Sparse Core Ops, SparseCore 0:
  23.9 14.8 all-gather.8
  43.4 76.8 reduce-scatter.8
  131.0 30.4 all-gather.10
  164.9 29.4 reduce-scatter.10
  195.8 16.6 all-gather.16
  214.5 16.6 all-gather.12
  233.6 110.7 reduce-scatter.16
  346.7 212.3 reduce-scatter.12
  564.9 116.3 all-gather.18
  689.9 29.3 reduce-scatter.18
  736.9 13.9 all-gather.20
  754.4 43.6 reduce-scatter.20
  826.9 44.8 all-gather.22
  873.8 62.2 all-gather.14
  939.0 29.8 reduce-scatter.22
  971.8 31.3 reduce-scatter.14
  1006.8 153.7 all-reduce.3
where the time goes:
time: 1180 us
  waiting for transfers between devices  929 us (79%)
  blocking collectives  87.3 us (7%)
  matrix products  69.7 us (6%)
  other arithmetic  37.9 us (3%)
  local copies, waits for them, and re-layouts  37.7 us (3%)
  between operations  14.6 us (1%)
    reduce_scatter x4, waiting for transfers between devices, row_product(): lax.psum_scatter(matrix_result(gathered, weight, flipped), 'row', scatter...  431 us
    all_gather x4, waiting for transfers between devices, gather_rows(): return lax.all_gather(piece, 'row', axis=0, tiled=True)  251 us
    psum x1, waiting for transfers between devices, per_device(): lax.psum(grad_joint.astype(jnp.bfloat16), 'dp').astype(jnp.float32)  138 us
    reduce_scatter x4, waiting for transfers between devices, col_sum(): lax.psum_scatter(matrix_result(gathered, weight, flipped), 'col', scatter...  66.9 us
    psum x4, blocking collectives, row_stats(): return lax.psum(partial_value, 'row')  49.7 us
    all_gather x4, waiting for transfers between devices, gather_cols(): return lax.all_gather(piece, 'col', axis=0, tiled=True)  39.9 us
    psum x1, blocking collectives, per_device(): lax.psum((gain_in_full, gain_mid_full, gain_query, gain_key), ('dp', 'row...  37.7 us
    dot_general x4, matrix products, matrix_result(): return jnp.dot(left, right, preferred_element_type=jnp.float32)  23.7 us
  transfers between devices with their start and end apart: 17, of which 16 were waited for; matrix products, arithmetic and copies ran while one was open for 5% of the time, Pallas kernels for 0%

commit v1 on v0

--- a/solution.py
+++ b/solution.py
@@ -7,6 +7,27 @@
 HEAD_SIZE = 128
 EPSILON = 1e-06
 THETA = 1000000.0
+
+
+def keep_up_local_data(base_x, axis_name):
+    answer, heard, value_now = (lax.psum(1, axis_name), lax.axis_index(axis_name), base_x.shape[0])
+    blocks_here = tuple(((j, (j + 1) % answer) for j in range(answer)))
+    state_now = jnp.zeros((*base_x.shape[:0], answer * value_now, *base_x.shape[1:]), base_x.dtype)
+    state_now = lax.dynamic_update_slice_in_dim(state_now, base_x, heard * value_now, axis=0)
+    upper = mat_out = base_x
+    raw_out = answer // 2
+    log = tuple(((j, (j - 1) % answer) for j in range(answer)))
+    for no in range(1, raw_out + 1):
+        upper = lax.ppermute(upper, axis_name, perm=blocks_here)
+        state_now = lax.dynamic_update_slice_in_dim(
+            state_now, upper, (heard - no) % answer * value_now, axis=0
+        )
+        if no < answer - raw_out:
+            mat_out = lax.ppermute(mat_out, axis_name=axis_name, perm=log)
+            state_now = lax.dynamic_update_slice_in_dim(
+                state_now, mat_out, (heard + no) % answer * value_now, axis=0
+            )
+    return state_now
 
 
 def positions_of(segment):
@@ -161,7 +182,7 @@
 
 
 def gather_cols(piece):
-    return lax.all_gather(piece, "col", axis=0, tiled=True)
+    return keep_up_local_data(piece, "col")
 
 
 def gather_rows(piece):

time: 1180 us -> 1130 us (0.958)
  waiting for transfers between devices: 929 us -> 885 us
    ppermute x0 -> x12, waiting for transfers between devices: none -> 41.8 us  [the longest x8 41.7 us: keep_up_local_data(): upper = lax.ppermute(upper, axis_name, perm=blocks_here)]
    all_gather x4 -> x0, waiting for transfers between devices: 39.9 us -> none  [gather_cols(): return lax.all_gather(piece, 'col', axis=0, tiled=True)]
    reduce_scatter x4, waiting for transfers between devices: 431 us -> 403 us  [row_product(): lax.psum_scatter(matrix_result(gathered, weight, flipped), 'row', scatter...]
    reduce_scatter x4, waiting for transfers between devices: 66.9 us -> 49.4 us  [col_sum(): lax.psum_scatter(matrix_result(gathered, weight, flipped), 'col', scatter...]
  transfers between devices with their start and end apart: 17 -> 25, of which waited for: 16 -> 20; matrix products, arithmetic and copies ran while one was open for 5% -> 5% of each run, Pallas kernels for 0% -> 0%
where the time goes in v1:
time: 1130 us
  waiting for transfers between devices  885 us (78%)
  blocking collectives  87.5 us (8%)
  matrix products  63.4 us (6%)
  other arithmetic  36.9 us (3%)
  local copies, waits for them, and re-layouts  33.9 us (3%)
  between operations  14.8 us (1%)
    reduce_scatter x4, waiting for transfers between devices, row_product(): lax.psum_scatter(matrix_result(gathered, weight, flipped), 'row', scatter...  403 us
    all_gather x4, waiting for transfers between devices, gather_rows(): return lax.all_gather(piece, 'row', axis=0, tiled=True)  251 us
    psum x1, waiting for transfers between devices, per_device(): lax.psum(grad_joint.astype(jnp.bfloat16), 'dp').astype(jnp.float32)  139 us
    psum x4, blocking collectives, row_stats(): return lax.psum(partial_value, 'row')  49.8 us
    reduce_scatter x4, waiting for transfers between devices, col_sum(): lax.psum_scatter(matrix_result(gathered, weight, flipped), 'col', scatter...  49.4 us
    ppermute x8, waiting for transfers between devices, keep_up_local_data(): upper = lax.ppermute(upper, axis_name, perm=blocks_here)  41.7 us
    psum x1, blocking collectives, per_device(): lax.psum((gain_in_full, gain_mid_full, gain_query, gain_key), ('dp', 'row...  37.7 us
  transfers between devices with their start and end apart: 25, of which 20 were waited for; matrix products, arithmetic and copies ran while one was open for 5% of the time, Pallas kernels for 0%

profile of v1, /device:TPU:0, one launch (start us, length us, event | category | flops | bytes accessed | tf_op | source)
XLA Modules:
  0.0 1129.1 jit_solution(3919943872734848518)
XLA Ops:
  8.5 13.5 %psum.84 = f32[256]{0:T(256)S(1)} all-reduce(f32[256]{0:T(256)S(1)} %fusion.21), channel_id=1, replica_groups=mesh['dp'=2,'row'=4,'col'=4] {'row'}, use_global_device_ids=true, to_apply=%region_1.2 | all-reduce | flops 256 | bytes 2048 | tf_op jit(solution)/shard_map/psum | solution.py:181
  44.4 73.5 %reduce-scatter.9.cloned.1.call-done = f32[256,1024]{1,0:T(8,128)} async-done(((f32[1024,1024]{1,0:T(8,128)}), f32[256,1024]{1,0:T(8,128)}) %reduce-scatter.9.cloned.1.call-update) | async-done | bytes 1048592 | tf_op jit(solution)/shard_map/reduce_scatter | solution.py:193
  125.1 30.5 %all-gather.5.cloned.1.call-done = bf16[1024,512]{0,1:T(8,128)(2,1)} async-done(((bf16[256,512]{0,1:T(8,128)(2,1)}), bf16[1024,512]{0,1:T(8,128)(2,1)}) %all-gather.5.cloned.1.call-update) | async-done | bytes 1048592 | tf_op jit(solution)/shard_map/all_gather | solution.py:189
  160.9 5.9 collective-permute-done.6
  167.0 5.6 collective-permute-done.8
  178.1 10.6 reduce-scatter.11.cloned.1.call-done
  189.9 12.3 %psum.85 = f32[256]{0:T(256)} all-reduce(f32[256]{0:T(256)S(1)} %get-tuple-element.85), channel_id=1, replica_groups=mesh['dp'=2,'row'=4,'col'=4] {'row'}, use_global_device_ids=true, to_apply=%region_11.12 | all-reduce | flops 256 | bytes 2048 | tf_op jit(solution)/shard_map/psum | solution.py:181
  217.6 6.4 fusion.52
  224.3 77.5 %reduce-scatter.17.cloned.1.call-done = f32[256,1536]{1,0:T(8,128)} async-done(((f32[1024,1536]{1,0:T(8,128)}), f32[256,1536]{1,0:T(8,128)}) %reduce-scatter.17.cloned.1.call-update) | async-done | bytes 1572880 | tf_op jit(solution)/shard_map/reduce_scatter | solution.py:193
  301.8 214.5 %reduce-scatter.13.cloned.1.call-done = f32[256,3072]{1,0:T(8,128)} async-done(((f32[1024,3072]{1,0:T(8,128)}), f32[256,3072]{1,0:T(8,128)}) %reduce-scatter.13.cloned.1.call-update) | async-done | bytes 3145744 | tf_op jit(solution)/shard_map/reduce_scatter | solution.py:193
  522.0 116.4 %all-gather.9.cloned.1.call-done = bf16[1024,3072]{1,0:T(8,128)(2,1)} async-done(((bf16[256,3072]{1,0:T(8,128)(2,1)}), bf16[1024,3072]{1,0:T(8,128)(2,1)}) %all-gather.9.cloned.1.call-update) | async-done | bytes 6291472 | tf_op jit(solution)/shard_map/all_gather | solution.py:189
  638.4 8.5 fusion.55
  647.0 29.5 %reduce-scatter.19.cloned.1.call-done = f32[256,512]{1,0:T(8,128)} async-done(((f32[1024,512]{1,0:T(8,128)}), f32[256,512]{1,0:T(8,128)}) %reduce-scatter.19.cloned.1.call-update) | async-done | bytes 524304 | tf_op jit(solution)/shard_map/reduce_scatter | solution.py:199
  678.3 12.4 %psum.86 = f32[256]{0:T(256)} all-reduce(f32[256]{0:T(256)} %get-tuple-element.57), channel_id=1, replica_groups=mesh['dp'=2,'row'=4,'col'=4] {'row'}, use_global_device_ids=true, to_apply=%region_17.18 | all-reduce | flops 256 | bytes 2048 | tf_op jit(solution)/shard_map/psum | solution.py:181
  694.6 6.0 collective-permute-done.9
  700.7 5.7 collective-permute-done.11
  712.8 37.7 %reduce-scatter.21.cloned.1.call-done = f32[256,512]{1,0:T(8,128)} async-done(((f32[1024,512]{1,0:T(8,128)}), f32[256,512]{1,0:T(8,128)}) %reduce-scatter.21.cloned.1.call-update) | async-done | bytes 524304 | tf_op jit(solution)/shard_map/reduce_scatter | solution.py:193
  779.1 44.2 %all-gather.11.cloned.1.call-done = bf16[1024,1024]{1,0:T(8,128)(2,1)} async-done(((bf16[256,1024]{1,0:T(8,128)(2,1)}), bf16[1024,1024]{1,0:T(8,128)(2,1)}) %all-gather.11.cloned.1.call-update) | async-done | bytes 2097168 | tf_op jit(solution)/shard_map/all_gather | solution.py:189
  827.8 59.7 %all-gather.7.cloned.1.call-done = bf16[1024,1536]{1,0:T(8,128)(2,1)} async-done(((bf16[256,1536]{1,0:T(8,128)(2,1)}), bf16[1024,1536]{1,0:T(8,128)(2,1)}) %all-gather.7.cloned.1.call-update) | async-done | bytes 3145744 | tf_op jit(solution)/shard_map/all_gather | solution.py:189
  898.2 7.8 convolution_convert_fusion
  911.2 9.3 reduce-scatter.23.cloned.1.call-done
  922.1 11.6 %psum.87 = f32[256]{0:T(256)S(1)} all-reduce(f32[256]{0:T(256)S(1)} %get-tuple-element.59), channel_id=1, replica_groups=mesh['dp'=2,'row'=4,'col'=4] {'row'}, use_global_device_ids=true, to_apply=%region_24.25 | all-reduce | flops 256 | bytes 2048 | tf_op jit(solution)/shard_map/psum | solution.py:181
  933.8 37.7 %all-reduce = (f32[2048]{0:T(1024)}, f32[2048]{0:T(1024)}, f32[128]{0:T(128)}, f32[128]{0:T(128)}) all-reduce(f32[2048]{0:T(1024)S(1)} %dynamic_update_slice.79, f32[2048]{0:T(1024)S(1)} %dynamic_update_slice.80, f32[128]{0:T(128)S(1)} %bitcast_reduce_fusion, ...), channel_id=1, replica_groups=mesh['dp'=2,'row'=4,'col'=4] {'dp','row','col'}, use_global_device_ids=true, to_apply=%region_30.31 | all-reduce | flops 4352 | bytes 34816 | tf_op jit(solution)/shard_map/psum | solution.py:324
  973.8 138.6 %all-reduce.4.cloned.1.call-done = (bf16[512,1024]{1,0:T(8,128)(2,1)}, bf16[512,512]{1,0:T(8,128)(2,1)}, bf16[512,3072]{1,0:T(8,128)(2,1)}, bf16[1536,512]{1,0:T(8,128)(2,1)}) async-done(((bf16[512,1024]{1,0:T(8,128)(2,1)}, bf16[512,512]{1,0:T(8,128)(2,1)}, bf16[512,3072]{1,0:T(8,128)(2,1)}, bf16[1536,512]{1,0:T(8,128)(2,1)}), (bf16[512,1024]{1,0:T(8,128)(2,1)}, bf16[512,512]{1,0:T(8,128)(2,1)}, ...) | async-done | bytes 6291472 | tf_op jit(solution)/shard_map/psum | solution.py:308
  (293 shorter events, 138.8 us)
Async XLA Ops:
  7.2 110.7 %reduce-scatter.9.cloned.1.call-start = ((), (), s32[]{:S(2)}) async-start(), calls=%async_computation.8 | async-start | bytes 5242880 | tf_op jit(solution)/shard_map/reduce_scatter | solution.py:193
  23.9 7.0 collective-permute-start
  24.0 8.0 collective-permute-start.1
  41.6 113.9 %all-gather.5.cloned.1.call-start = ((), (), s32[]{:S(2)}) async-start(), calls=%async_computation.9 | async-start | bytes 1310720 | tf_op jit(solution)/shard_map/all_gather | solution.py:189
  125.0 63.7 %reduce-scatter.11.cloned.1.call-start = ((), (), s32[]{:S(2)}) async-start(), calls=%async_computation.10 | async-start | bytes 2621440 | tf_op jit(solution)/shard_map/reduce_scatter | solution.py:199
  159.0 142.7 %reduce-scatter.17.cloned.1.call-start = ((), (), s32[]{:S(2)}) async-start(), calls=%async_computation.14 | async-start | bytes 7864320 | tf_op jit(solution)/shard_map/reduce_scatter | solution.py:193
  159.1 7.7 collective-permute-start.6
  159.2 7.7 collective-permute-start.7
  166.8 5.8 collective-permute-start.8
  178.0 338.3 %reduce-scatter.13.cloned.1.call-start = ((), (), s32[]{:S(2)}) async-start(), calls=%async_computation.11 | async-start | bytes 15728640 | tf_op jit(solution)/shard_map/reduce_scatter | solution.py:193
  203.3 7.6 collective-permute-start.3
  203.8 7.2 collective-permute-start.4
  210.8 5.8 collective-permute-start.5
  224.0 414.4 %all-gather.9.cloned.1.call-start = ((), (), s32[]{:S(2)}) async-start(), calls=%async_computation.15 | async-start | bytes 7864320 | tf_op jit(solution)/shard_map/all_gather | solution.py:189
  521.9 154.5 %reduce-scatter.19.cloned.1.call-start = ((), (), s32[]{:S(2)}) async-start(), calls=%async_computation.16 | async-start | bytes 2621440 | tf_op jit(solution)/shard_map/reduce_scatter | solution.py:199
  646.9 103.6 %reduce-scatter.21.cloned.1.call-start = ((), (), s32[]{:S(2)}) async-start(), calls=%async_computation.17 | async-start | bytes 2621440 | tf_op jit(solution)/shard_map/reduce_scatter | solution.py:193
  692.8 7.8 collective-permute-start.9
  692.8 7.8 collective-permute-start.10
  700.6 5.8 collective-permute-start.11
  709.5 113.8 %all-gather.11.cloned.1.call-start = ((), (), s32[]{:S(2)}) async-start(), calls=%async_computation.18 | async-start | bytes 2621440 | tf_op jit(solution)/shard_map/all_gather | solution.py:189
  778.3 109.3 %all-gather.7.cloned.1.call-start = ((), (), s32[]{:S(2)}) async-start(), calls=%async_computation.12 | async-start | bytes 3932160 | tf_op jit(solution)/shard_map/all_gather | solution.py:189
  778.9 141.7 %reduce-scatter.23.cloned.1.call-start = ((), (), s32[]{:S(2)}) async-start(), calls=%async_computation.19 | async-start | bytes 2621440 | tf_op jit(solution)/shard_map/reduce_scatter | solution.py:199
  827.8 143.7 %reduce-scatter.15.cloned.1.call-start = ((), (), s32[]{:S(2)}) async-start(), calls=%async_computation.13 | async-start | bytes 2621440 | tf_op jit(solution)/shard_map/reduce_scatter | solution.py:199
  892.6 219.9 %all-reduce.4.cloned.1.call-start = ((), (), s32[]{:S(2)}) async-start(), calls=%async_computation.20 | async-start | bytes 12582912 | tf_op jit(solution)/shard_map/psum | solution.py:308
  (66 other events, 1282.9 us)
Sparse Core Ops, SparseCore 0:
  41.8 76.0 reduce-scatter.8
  125.1 30.4 all-gather.4
  159.2 29.4 reduce-scatter.10
  190.9 110.8 reduce-scatter.16
  304.0 212.2 reduce-scatter.12
  522.0 116.3 all-gather.8
  647.0 29.3 reduce-scatter.18
  709.6 40.8 reduce-scatter.20
  778.4 44.8 all-gather.10
  825.3 62.2 all-gather.6
  890.7 29.8 reduce-scatter.22
  923.5 31.3 reduce-scatter.14
  958.6 153.7 all-reduce.3
